TPU v7x, 32 devices: a whole 2x2x4 slice. The times are simulated.
32 devices in a mesh: orb: 8 (over y, x, core), walk: 4 (over z).
Axes of the slice: x: 2, y: 2, z: 4, core: 2. Of those that a mesh axis runs over, the one named last changes fastest.
Arguments:
- chol: bfloat16 [32, 2048, 2048], P(None, 'orb', 'walk'), may hold values from -6 to 6
- orbitals: bfloat16 [2048, 1024], replicated, may hold values from -0.125 to 0.125
- greens: bfloat16 [4, 1024, 2048], P('walk'), may hold values from -0.00390625 to 0.00390625
- shift: float32 [32], P('orb'), may hold values from -6 to 6
Outputs:
- force_bias: float32 [4, 32], P('walk', 'orb')
- rotated: bfloat16 [32, 1024, 2048], P('orb', None, 'walk')
All inputs are finite; a program needn't handle non-finite values.
Results may differ from a plain program's by a relative error of at most 0.007.
Values may be sent and summed in bfloat16 or wider, within the bound.
A program may use at most 64 MiB of HBM per device.

v0:
```python
import jax
import jax.numpy as jnp
from jax import lax
from jax.sharding import PartitionSpec as P


def local(chol, orbitals, greens, shift):
    regrouped = lax.all_to_all(chol, "orb", split_axis=0, concat_axis=1, tiled=True)
    rotation = jnp.einsum("pi,gpq->giq", orbitals, regrouped, preferred_element_type=jnp.float32)
    rotated = rotation.astype(jnp.bfloat16)
    row_count = chol.shape[1]
    row_start = lax.axis_index("orb") * row_count
    orbital_rows = lax.dynamic_slice_in_dim(orbitals, row_start, row_count, 0)
    products = jnp.einsum("pi,wiq->wpq", orbital_rows, greens, preferred_element_type=jnp.float32)
    arrived = lax.all_to_all(
        products.astype(jnp.bfloat16), "walk", split_axis=2, concat_axis=0, tiled=True
    ).astype(products.dtype)
    terms = jnp.einsum(
        "wpq,gpq->wg", arrived, chol.astype(jnp.float32), precision=lax.Precision.HIGHEST
    )
    by_vector = lax.psum_scatter(terms, "orb", scatter_dimension=1, tiled=True)
    totals = lax.psum_scatter(by_vector, "walk", scatter_dimension=0, tiled=True)
    return (totals - shift[None, :], rotated)


def solution(mesh):
    in_specs = (P(None, "orb", "walk"), P(), P("walk", None, None), P("orb"))
    out_specs = (P("walk", "orb"), P("orb", None, "walk"))
    return jax.shard_map(local, mesh=mesh, in_specs=in_specs, out_specs=out_specs, check_vma=False)
```

profile of v0, /device:TPU:0, one launch (start us, length us, event | category | flops | bytes accessed | tf_op | source)
XLA Modules:
  0.0 214.4 jit_solution(16381867713157282100)
XLA Ops:
  0.6 3.6 %fusion.11 = bf16[1,256,2048]{2,1,0:T(8,128)(2,1)S(1)} fusion(bf16[1,1024,2048]{2,1,0:T(8,128)(2,1)} %param.6, bf16[2048,1024]{1,0:T(8,128)(2,1)} %param.5, s32[]{:T(128)S(6)} %select_n.3), kind=kOutput, calls=%fused_computation.8 | convolution fusion | flops 1074266112 | bytes 5767172 | tf_op jit(solution)/shard_map/pi,wiq->wpq/dot_general | solution.py:14
  4.3 1.7 copy.9
  5.9 0.5 broadcast
  6.5 10.6 %reduce = bf16[2048,256]{1,0:T(8,128)(2,1)S(1)} reduce(bf16[2048,1,256]{2,1,0:T(2,128)(2,1)S(1)} %bitcast.45, bf16[]{:T(256)} %broadcast), dimensions={1}, to_apply=%bitcast.40.reduce_sub_computation | reduce | bytes 2097154
  17.1 0.3 reshape.17
  17.4 31.9 %all_to_all.36 = bf16[4,2,65536]{2,1,0:T(2,128)(2,1)S(1)} all-to-all(bf16[4,2,65536]{2,1,0:T(2,128)(2,1)S(1)} %reshape.17), channel_id=1, replica_groups=mesh['orb'=8,'walk'=4] {'walk'}, dimensions={0} | all-to-all | bytes 2097152 | tf_op jit(solution)/shard_map/all_to_all | solution.py:15
  49.3 0.0 copy-start.2
  49.3 0.0 copy-start.1
  49.3 5.4 %all-to-all-start.1 = ((bf16[32,256,512]{2,1,0:T(8,128)(2,1)}), bf16[32,256,512]{2,1,0:T(8,128)(2,1)}, u32[]{:S(2)}, u32[]{:S(2)}) async-start(bf16[32,256,512]{2,1,0:T(8,128)(2,1)} %param.4), calls=%async_computation.1 | async-start | bytes 16777216 | tf_op jit(solution)/shard_map/all_to_all | solution.py:8
  54.6 0.0 copy-done.2
  54.7 0.6 dynamic-slice
  55.2 0.0 copy-done.1
  55.2 0.6 dynamic-slice.2
  56.5 1.0 reshape.18
  57.5 0.2 copy.16
  57.6 1.0 copy.14
  58.7 0.0 copy-start
  58.7 13.1 %fusion.14 = f32[4,32]{1,0:T(4,128)S(1)} fusion(bf16[32,256,512]{2,1,0:T(8,128)(2,1)} %param.4, bf16[1,256,4,512]{3,2,1,0:T(4,128)(2,1)S(1)} %copy.14), kind=kOutput, calls=%fused_computation.9 | convolution fusion | flops 33554432 | bytes 9437696 | tf_op jit(solution)/shard_map/wpq,gpq->wg/dot_general | solution.py:18
  71.7 83.1 %all-reduce = f32[4,32]{1,0:T(4,128)S(1)} all-reduce(f32[4,32]{1,0:T(4,128)S(1)} %fusion.14), channel_id=2, replica_groups=mesh['orb'=8,'walk'=4] {'orb'}, use_global_device_ids=true, to_apply=%region_0.0.clone | all-reduce | flops 128 | bytes 1024
  154.9 0.1 constant_dynamic-slice_fusion.1
  154.9 10.0 %all-reduce.1 = f32[4,4]{1,0:T(4,128)S(1)} all-reduce(f32[4,4]{1,0:T(4,128)S(1)} %constant_dynamic-slice_fusion.1), channel_id=3, replica_groups=mesh['orb'=8,'walk'=4] {'walk'}, use_global_device_ids=true, to_apply=%region_1.0.clone | all-reduce | flops 16 | bytes 128
  164.9 0.0 copy-done
  164.9 1.2 fusion.19
  166.1 0.0 all-to-all-done.1
  166.1 14.8 %copy.12 = bf16[8,4,256,512]{2,0,3,1:T(8,128)(2,1)} copy(bf16[8,4,256,512]{3,2,1,0:T(8,128)(2,1)} %bitcast.8) | data formatting | bytes 16777216 | tf_op jit(solution)/shard_map/all_to_all | solution.py:8
  180.9 13.5 %all_to_all.33 = bf16[4,2048,512]{1,2,0:T(8,128)(2,1)} reshape(bf16[4,8,256,512]{2,1,3,0:T(8,128)(2,1)} %bitcast.43) | data formatting | bytes 16777216 | tf_op jit(solution)/shard_map/all_to_all | solution.py:8
  194.4 13.8 %convert_bitcast_fusion = bf16[4,1024,512]{1,2,0:T(8,128)(2,1)} fusion(bf16[4,2048,512]{1,2,0:T(8,128)(2,1)} %all_to_all.33, bf16[2048,1024]{1,0:T(8,128)(2,1)} %param.5), kind=kOutput, calls=%fused_computation.6 | convolution fusion | flops 8592031744 | bytes 16777216 | tf_op jit(solution)/shard_map/pi,gpq->giq/dot_general | solution.py:9
  208.2 6.2 %copy.13 = bf16[4,1024,512]{2,1,0:T(8,128)(2,1)} copy(bf16[4,1024,512]{1,2,0:T(8,128)(2,1)} %convert_bitcast_fusion) | data formatting | bytes 8388608
Async XLA Ops:
  49.3 5.4 %copy-start.2 = (u32[32]{0:T(128)S(1)}, u32[32]{0:T(128)}, u32[]{:S(2)}) copy-start(u32[32]{0:T(128)} %constant.16) | copy-start | bytes 388
  49.3 6.0 %copy-start.1 = (u32[32]{0:T(128)S(1)}, u32[32]{0:T(128)}, u32[]{:S(2)}) copy-start(u32[32]{0:T(128)} %constant.20) | copy-start | bytes 388
  49.3 116.8 %all-to-all-start.1 = ((bf16[32,256,512]{2,1,0:T(8,128)(2,1)}), bf16[32,256,512]{2,1,0:T(8,128)(2,1)}, u32[]{:S(2)}, u32[]{:S(2)}) async-start(bf16[32,256,512]{2,1,0:T(8,128)(2,1)} %param.4), calls=%async_computation.1 | async-start | bytes 16777216 | tf_op jit(solution)/shard_map/all_to_all | solution.py:8
  58.7 106.3 %copy-start = (f32[4]{0:T(128)S(1)}, f32[4]{0:T(128)}, u32[]{:S(2)}) copy-start(f32[4]{0:T(128)} %param.7) | copy-start | bytes 52
where the time goes:
time: 215 us; the launch traced here: 214 us
  blocking collectives  125 us (58%)
  local copies, waits for them, and re-layouts  40.4 us (19%)
  matrix products  30.5 us (14%)
  other arithmetic  11.8 us (5%)
  starting transfers between devices  5.36 us (2%)
    unnamed x2, blocking collectives  93.1 us
    all_to_all x1, blocking collectives, local(): lax.all_to_all(products.astype(jnp.bfloat16), 'walk', split_axis=2, conca...  31.9 us
    all_to_all x2, local copies, waits for them, and re-layouts, local(): lax.all_to_all(chol, 'orb', split_axis=0, concat_axis=1, tiled=True)  28.3 us
    dot_general x1, matrix products, local(): jnp.einsum('pi,gpq->giq', orbitals, regrouped, preferred_element_type=jnp...  13.8 us
    dot_general x1, matrix products, local(): jnp.einsum('wpq,gpq->wg', arrived, chol.astype(jnp.float32), precision=la...  13.1 us
    unnamed x1, other arithmetic  10.6 us
    unnamed x14, local copies, waits for them, and re-layouts  9.43 us
    all_to_all x1, starting transfers between devices, local(): lax.all_to_all(chol, 'orb', split_axis=0, concat_axis=1, tiled=True)  5.36 us
  transfers between devices with their start and end apart: 1, of which 0 were waited for; matrix products, arithmetic and copies ran while one was open for 8% of the time, Pallas kernels for 0%

commit v1 on v0

v1 whole, which is shorter than its diff:
```python
import functools

import jax
import jax.numpy as jnp
from jax import lax
from jax.experimental import pallas as pl
from jax.experimental.pallas import tpu as pltpu
from jax.sharding import PartitionSpec as P

MESH = pl.DeviceIdType.MESH
LANES = 128


def xor(a, b, size):
    total, bit = 0, 1
    while bit < size:
        total = total + ((a // bit + b // bit) % 2) * bit
        bit *= 2
    return total


def kernel(
    n, m, chol, orbitals, greens, shift, bias_out, rotated,
    chunks, chol_v, orb_v, orb_t, greens_v, products, arrived, acc, rounded,
    terms, terms_in, sums, sums_in,
    local_sem, out_sem, send_sem, recv_sem, walk_send, walk_recv,
    term_send, term_recv, sum_send, sum_recv,
):
    me, my_walk = lax.axis_index("orb"), lax.axis_index("walk")
    vectors, rows, cols = chol.shape
    owned = vectors // n
    walkers = greens.shape[0]
    core = me % 2

    loads = [
        pltpu.make_async_copy(greens, greens_v, local_sem.at[0]),
        pltpu.make_async_copy(orbitals, orb_v, local_sem.at[1]),
        pltpu.make_async_copy(chol, chol_v, local_sem.at[2]),
    ]
    for load in loads:
        load.start()

    barrier = pltpu.get_barrier_semaphore()
    for k in range(1, n):
        pl.semaphore_signal(barrier, inc=1, device_id={"orb": xor(me, k, n)}, device_id_type=MESH)
    for k in range(1, m):
        pl.semaphore_signal(
            barrier, inc=1, device_id={"walk": (my_walk + k) % m}, device_id_type=MESH
        )
    pl.semaphore_wait(barrier, n + m - 2)

    def chunk_copy(g, k):
        peer = xor(me, k, n)
        return pltpu.make_async_remote_copy(
            src_ref=chol.at[peer * owned + g],
            dst_ref=chunks.at[k, g],
            send_sem=send_sem.at[k, g],
            recv_sem=recv_sem.at[k, g],
            device_id={"orb": peer},
            device_id_type=MESH,
        )

    def send_vector(g):
        half = n // 2
        for low in range(2):
            if low == 1:
                chunk_copy(g, 1).start()
            for high in range(1, half):
                chip = high + core * (half - 2 * high)
                chunk_copy(g, chip * 2 + low).start()

    early = max(owned - 1, 1)
    for g in range(early):
        send_vector(g)

    loads[0].wait()
    loads[1].wait()
    my_rows = orb_v[pl.ds(pl.multiple_of(me * rows, rows), rows), :]
    for w in range(walkers):
        for j in range(m):
            products[j, w] = jnp.dot(
                my_rows, greens_v[w, :, j * cols : (j + 1) * cols],
                preferred_element_type=jnp.float32,
            ).astype(products.dtype)

    def turn(s, _):
        orb_t[s] = orb_v[pl.ds(pl.multiple_of(s * rows, rows), rows), :].T
        return _

    lax.fori_loop(0, n, turn, 0)

    def walk_copy(k):
        peer = (my_walk + k) % m
        return pltpu.make_async_remote_copy(
            src_ref=products.at[peer],
            dst_ref=arrived.at[m - k],
            send_sem=walk_send.at[k],
            recv_sem=walk_recv.at[m - k],
            device_id={"walk": peer},
            device_id_type=MESH,
        )

    def walk_arrival(k):
        return pltpu.make_async_remote_copy(
            src_ref=products.at[0],
            dst_ref=arrived.at[k],
            send_sem=walk_send.at[k],
            recv_sem=walk_recv.at[k],
            device_id={"walk": (my_walk + k) % m},
            device_id_type=MESH,
        )

    for k in range(1, m):
        walk_copy(k).start()

    loads[2].wait()

    def begin(g, _):
        acc[g] = jnp.dot(orb_t[me], chol_v[me * owned + g], preferred_element_type=jnp.float32)
        return _

    lax.fori_loop(0, owned, begin, 0)
    arrived[0] = products[my_walk]
    for k in range(1, m):
        walk_arrival(k).wait_recv()

    def term(v, _):
        block = chol_v[v].astype(jnp.float32)
        for k in range(m):
            from_walk = (my_walk + k) % m
            for w in range(walkers):
                both = block * arrived[k, w].astype(jnp.float32)
                both = jnp.sum(both, axis=0, keepdims=True)
                part = both[:, :LANES]
                for start in range(LANES, cols, LANES):
                    part = part + both[:, start : start + LANES]
                terms[v // owned, from_walk, w, pl.ds(v % owned, 1), :] = part
        return _

    lax.fori_loop(0, vectors, term, 0)

    def take(g, k):
        chunk_copy(g, k).wait_recv()
        return acc[g] + jnp.dot(
            orb_t[xor(me, k, n)], chunks[k, g], preferred_element_type=jnp.float32
        )

    def add(g):
        def step(k, _):
            acc[g] = take(g, k)
            return _

        return step

    def write(g):
        return pltpu.make_async_copy(rounded.at[g], rotated.at[g], out_sem.at[g])

    def finish(g):
        rounded[g] = take(g, n - 1).astype(rounded.dtype)
        write(g).start()

    def term_copy(k):
        peer = xor(me, k, n)
        return pltpu.make_async_remote_copy(
            src_ref=terms.at[peer],
            dst_ref=terms_in.at[k],
            send_sem=term_send.at[k],
            recv_sem=term_recv.at[k],
            device_id={"orb": peer},
            device_id_type=MESH,
        )

    def sum_copy(k):
        peer = (my_walk + k) % m
        return pltpu.make_async_remote_copy(
            src_ref=sums.at[peer],
            dst_ref=sums_in.at[m - k],
            send_sem=sum_send.at[k],
            recv_sem=sum_recv.at[m - k],
            device_id={"walk": peer},
            device_id_type=MESH,
        )

    def sum_arrival(k):
        return pltpu.make_async_remote_copy(
            src_ref=sums.at[0],
            dst_ref=sums_in.at[k],
            send_sem=sum_send.at[k],
            recv_sem=sum_recv.at[k],
            device_id={"walk": (my_walk + k) % m},
            device_id_type=MESH,
        )

    lax.fori_loop(1, n - 1, add(0), 0)
    for k in range(1, n):
        term_copy(k).start()
    for g in range(early, owned):
        send_vector(g)
    if owned > 1:
        finish(0)

    if owned > 2:
        def vector(g, _):
            lax.fori_loop(1, n - 1, add(g), 0)
            finish(g)
            return _

        lax.fori_loop(1, owned - 1, vector, 0)

    mine = terms[me]
    for k in range(1, n):
        term_copy(k).wait_recv()
        mine = mine + terms_in[k]
    sums[...] = mine
    last = owned - 1
    if owned > 1:
        lax.fori_loop(1, 2, add(last), 0)
    for k in range(1, m):
        sum_copy(k).start()
    if owned > 1:
        lax.fori_loop(2, n - 1, add(last), 0)
    total = sums[my_walk]
    for k in range(1, m):
        sum_arrival(k).wait_recv()
        total = total + sums_in[k]
    bias_out[...] = jnp.sum(total, axis=-1) - shift[...]
    finish(last)

    for k in range(1, m):
        walk_copy(k).wait_send()
        sum_copy(k).wait_send()
    for k in range(1, n):
        term_copy(k).wait_send()

    def drain(g, _):
        def one(k, _):
            chunk_copy(g, k).wait_send()
            return _

        lax.fori_loop(1, n, one, 0)
        write(g).wait()
        return _

    lax.fori_loop(0, owned, drain, 0)


def local(n, m, chol, orbitals, greens, shift):
    vectors, rows, cols = chol.shape
    owned = vectors // n
    walkers, occupied, _ = greens.shape
    bf16, f32 = jnp.bfloat16, jnp.float32
    dma = pltpu.SemaphoreType.DMA
    any_space = pl.BlockSpec(memory_space=pl.ANY)
    vmem = pl.BlockSpec(memory_space=pltpu.VMEM)
    return pl.pallas_call(
        functools.partial(kernel, n, m),
        out_shape=(
            jax.ShapeDtypeStruct((walkers, owned), f32),
            jax.ShapeDtypeStruct((owned, occupied, cols), bf16),
        ),
        in_specs=[any_space, any_space, any_space, vmem],
        out_specs=(vmem, any_space),
        scratch_shapes=[
            pltpu.VMEM((n, owned, rows, cols), bf16),
            pltpu.VMEM(chol.shape, bf16),
            pltpu.VMEM(orbitals.shape, bf16),
            pltpu.VMEM((n, occupied, rows), bf16),
            pltpu.VMEM(greens.shape, bf16),
            pltpu.VMEM((m, walkers, rows, cols), bf16),
            pltpu.VMEM((m, walkers, rows, cols), bf16),
            pltpu.VMEM((owned, occupied, cols), f32),
            pltpu.VMEM((owned, occupied, cols), bf16),
            pltpu.VMEM((n, m, walkers, owned, LANES), f32),
            pltpu.VMEM((n, m, walkers, owned, LANES), f32),
            pltpu.VMEM((m, walkers, owned, LANES), f32),
            pltpu.VMEM((m, walkers, owned, LANES), f32),
            dma((3,)),
            dma((owned,)),
            dma((n, owned)),
            dma((n, owned)),
            dma((m,)),
            dma((m,)),
            dma((n,)),
            dma((n,)),
            dma((m,)),
            dma((m,)),
        ],
        compiler_params=pltpu.CompilerParams(
            collective_id=0, has_side_effects=True, vmem_limit_bytes=60 * 2**20
        ),
    )(chol, orbitals, greens, shift.reshape(1, owned))


def solution(mesh):
    in_specs = (P(None, "orb", "walk"), P(), P("walk", None, None), P("orb"))
    out_specs = (P("walk", "orb"), P("orb", None, "walk"))
    body = functools.partial(local, mesh.shape["orb"], mesh.shape["walk"])
    return jax.shard_map(body, mesh=mesh, in_specs=in_specs, out_specs=out_specs, check_vma=False)
```

time: 215 us -> 109 us (0.51)
  blocking collectives: 125 us -> 0 us
  Pallas kernels: 0 us -> 102 us
  local copies, waits for them, and re-layouts: 40.4 us -> 5.61 us
  matrix products: 30.5 us -> 0 us
  other arithmetic: 11.8 us -> 0 us
  starting transfers between devices: 5.36 us -> 0 us
    pallas_call x0 -> x1, Pallas kernels: none -> 102 us  [local(): pl.pallas_call(functools.partial(kernel, n, m), out_shape=(jax.ShapeDtype...]
    unnamed x2 -> x0, blocking collectives: 93.1 us -> none
    all_to_all x1 -> x0, blocking collectives: 31.9 us -> none  [local(): lax.all_to_all(products.astype(jnp.bfloat16), 'walk', split_axis=2, conca...]
    dot_general x3 -> x0, matrix products: 30.5 us -> none  [the longest x1 13.8 us: local(): jnp.einsum('pi,gpq->giq', orbitals, regrouped, preferred_element_type=jnp...]
    all_to_all x3 -> x0, local copies, waits for them, and re-layouts: 29.3 us -> none  [the longest x2 28.3 us: local(): lax.all_to_all(chol, 'orb', split_axis=0, concat_axis=1, tiled=True)]
    unnamed x1 -> x0, other arithmetic: 10.6 us -> none
    all_to_all x1 -> x0, starting transfers between devices: 5.36 us -> none  [local(): lax.all_to_all(chol, 'orb', split_axis=0, concat_axis=1, tiled=True)]
    unnamed x14 -> x2, local copies, waits for them, and re-layouts: 9.43 us -> 5.61 us
  transfers between devices with their start and end apart: 1 -> 0, of which waited for: 0 -> 0; matrix products, arithmetic and copies ran while one was open for 8% -> 0% of each run, Pallas kernels for 0% -> 0%
where the time goes in v1:
time: 109 us
  Pallas kernels  102 us (94%)
  local copies, waits for them, and re-layouts  5.61 us (5%)
    pallas_call x1, Pallas kernels, local(): pl.pallas_call(functools.partial(kernel, n, m), out_shape=(jax.ShapeDtype...  102 us
    unnamed x2, local copies, waits for them, and re-layouts  5.61 us

profile of v1, /device:TPU:0, one launch (start us, length us, event | category | flops | bytes accessed | tf_op | source)
XLA Modules:
  0.0 108.7 jit_solution(15733985273076695567)
XLA Ops:
  0.6 102.4 %shard_map.59 = (f32[1,4]{1,0:T(1,128)}, bf16[4,1024,512]{2,1,0:T(8,128)(2,1)}) custom-call(bf16[32,256,512]{2,1,0:T(8,128)(2,1)} %chol.1, bf16[2048,1024]{1,0:T(8,128)(2,1)} %orbitals.1, bf16[1,1024,2048]{2,1,0:T(8,128)(2,1)} %greens.1, f32[1,4]{1,0:T(1,128)} %bitcast.1), custom_call_target="tpu_custom_call" | custom-call | tf_op jit(solution)/shard_map/pallas_call | solution.py:255
  103.1 1.1 %copy.8 = f32[1,4]{1,0:T(1,128)} copy(f32[1,4]{1,0:T(1,128)} %get-tuple-element.4) | data formatting | bytes 32
  104.2 4.5 %copy.9 = bf16[4,1024,512]{2,1,0:T(8,128)(2,1)} copy(bf16[4,1024,512]{2,1,0:T(8,128)(2,1)} %get-tuple-element.5) | data formatting | bytes 8388608

commit v2 on v1

--- a/solution.py
+++ b/solution.py
@@ -20,10 +20,10 @@
 
 
 def kernel(
-    n, m, chol, orbitals, greens, shift, bias_out, rotated,
-    chunks, chol_v, orb_v, orb_t, greens_v, products, arrived, acc, rounded,
+    n, m, chol, orbitals, greens, bias_out, rotated,
+    chunks, chol_v, orb_v, orb_t, greens_v, products, arrived, acc,
     terms, terms_in, sums, sums_in,
-    local_sem, out_sem, send_sem, recv_sem, walk_send, walk_recv,
+    local_sem, send_sem, recv_sem, walk_send, walk_recv,
     term_send, term_recv, sum_send, sum_recv,
 ):
     me, my_walk = lax.axis_index("orb"), lax.axis_index("walk")
@@ -37,8 +37,6 @@
         pltpu.make_async_copy(orbitals, orb_v, local_sem.at[1]),
         pltpu.make_async_copy(chol, chol_v, local_sem.at[2]),
     ]
-    for load in loads:
-        load.start()
 
     barrier = pltpu.get_barrier_semaphore()
     for k in range(1, n):
@@ -73,6 +71,8 @@
     for g in range(early):
         send_vector(g)
 
+    for load in loads:
+        load.start()
     loads[0].wait()
     loads[1].wait()
     my_rows = orb_v[pl.ds(pl.multiple_of(me * rows, rows), rows), :]
@@ -152,12 +152,8 @@
 
         return step
 
-    def write(g):
-        return pltpu.make_async_copy(rounded.at[g], rotated.at[g], out_sem.at[g])
-
     def finish(g):
-        rounded[g] = take(g, n - 1).astype(rounded.dtype)
-        write(g).start()
+        rotated[g] = take(g, n - 1).astype(rotated.dtype)
 
     def term_copy(k):
         peer = xor(me, k, n)
@@ -207,12 +203,25 @@
 
         lax.fori_loop(1, owned - 1, vector, 0)
 
+    def drain(g, _):
+        def one(k, _):
+            chunk_copy(g, k).wait_send()
+            return _
+
+        return lax.fori_loop(1, n, one, _)
+
+    last = owned - 1
+    lax.fori_loop(0, last, drain, 0)
+    for k in range(1, m):
+        walk_copy(k).wait_send()
+    for k in range(1, n):
+        term_copy(k).wait_send()
+
     mine = terms[me]
     for k in range(1, n):
         term_copy(k).wait_recv()
         mine = mine + terms_in[k]
     sums[...] = mine
-    last = owned - 1
     if owned > 1:
         lax.fori_loop(1, 2, add(last), 0)
     for k in range(1, m):
@@ -223,25 +232,24 @@
     for k in range(1, m):
         sum_arrival(k).wait_recv()
         total = total + sums_in[k]
-    bias_out[...] = jnp.sum(total, axis=-1) - shift[...]
+    bias_out[...] = jnp.sum(total, axis=-1)
     finish(last)
 
     for k in range(1, m):
-        walk_copy(k).wait_send()
         sum_copy(k).wait_send()
-    for k in range(1, n):
-        term_copy(k).wait_send()
-
-    def drain(g, _):
-        def one(k, _):
-            chunk_copy(g, k).wait_send()
-            return _
-
-        lax.fori_loop(1, n, one, 0)
-        write(g).wait()
-        return _
-
-    lax.fori_loop(0, owned, drain, 0)
+    drain(last, 0)
+
+
+def store(bias, shift, rounded, bias_out, rotated, sems):
+    writes = [
+        pltpu.make_async_copy(rounded.at[g], rotated.at[g], sems.at[g])
+        for g in range(rounded.shape[0])
+    ]
+    for write in writes:
+        write.start()
+    bias_out[...] = bias[...] - shift[...]
+    for write in writes:
+        write.wait()
 
 
 def local(n, m, chol, orbitals, greens, shift):
@@ -252,14 +260,14 @@
     dma = pltpu.SemaphoreType.DMA
     any_space = pl.BlockSpec(memory_space=pl.ANY)
     vmem = pl.BlockSpec(memory_space=pltpu.VMEM)
-    return pl.pallas_call(
+    bias, rounded = pl.pallas_call(
         functools.partial(kernel, n, m),
         out_shape=(
-            jax.ShapeDtypeStruct((walkers, owned), f32),
-            jax.ShapeDtypeStruct((owned, occupied, cols), bf16),
+            pltpu.VMEM((walkers, owned), f32),
+            pltpu.VMEM((owned, occupied, cols), bf16),
         ),
-        in_specs=[any_space, any_space, any_space, vmem],
-        out_specs=(vmem, any_space),
+        in_specs=[any_space] * 3,
+        out_specs=(vmem, vmem),
         scratch_shapes=[
             pltpu.VMEM((n, owned, rows, cols), bf16),
             pltpu.VMEM(chol.shape, bf16),
@@ -269,13 +277,11 @@
             pltpu.VMEM((m, walkers, rows, cols), bf16),
             pltpu.VMEM((m, walkers, rows, cols), bf16),
             pltpu.VMEM((owned, occupied, cols), f32),
-            pltpu.VMEM((owned, occupied, cols), bf16),
             pltpu.VMEM((n, m, walkers, owned, LANES), f32),
             pltpu.VMEM((n, m, walkers, owned, LANES), f32),
             pltpu.VMEM((m, walkers, owned, LANES), f32),
             pltpu.VMEM((m, walkers, owned, LANES), f32),
             dma((3,)),
-            dma((owned,)),
             dma((n, owned)),
             dma((n, owned)),
             dma((m,)),
@@ -286,9 +292,20 @@
             dma((m,)),
         ],
         compiler_params=pltpu.CompilerParams(
-            collective_id=0, has_side_effects=True, vmem_limit_bytes=60 * 2**20
+            collective_id=0, has_side_effects=True, vmem_limit_bytes=59 * 2**20
         ),
-    )(chol, orbitals, greens, shift.reshape(1, owned))
+    )(chol, orbitals, greens)
+    return pl.pallas_call(
+        store,
+        out_shape=(
+            jax.ShapeDtypeStruct((walkers, owned), f32),
+            jax.ShapeDtypeStruct((owned, occupied, cols), bf16),
+        ),
+        in_specs=[vmem, vmem, vmem],
+        out_specs=(vmem, any_space),
+        scratch_shapes=[dma((owned,))],
+        compiler_params=pltpu.CompilerParams(vmem_limit_bytes=2**20),
+    )(bias, shift.reshape(1, owned), rounded)
 
 
 def solution(mesh):

time: 109 us -> 104 us (0.954)
  local copies, waits for them, and re-layouts: 5.61 us -> 0.01 us
    unnamed x2, local copies, waits for them, and re-layouts: 5.61 us -> 0.01 us
    pallas_call x1 -> x2, Pallas kernels: 102 us -> 103 us  [the longest x1 100 us: local(): pl.pallas_call(functools.partial(kernel, n, m), out_shape=(pltpu.VMEM((wa...]
where the time goes in v2:
time: 104 us
  Pallas kernels  103 us (99%)
    pallas_call x1, Pallas kernels, local(): pl.pallas_call(functools.partial(kernel, n, m), out_shape=(pltpu.VMEM((wa...  100 us
    pallas_call x1, Pallas kernels, local(): pl.pallas_call(store, out_shape=(jax.ShapeDtypeStruct((walkers, owned), f...  2.55 us

profile of v2, /device:TPU:0, one launch (start us, length us, event | category | flops | bytes accessed | tf_op | source)
XLA Modules:
  0.0 103.6 jit_solution(16719984597222007710)
XLA Ops:
  0.6 0.0 copy-start
  0.6 100.4 %shard_map.59 = (f32[1,4]{1,0:T(1,128)S(1)}, bf16[4,1024,512]{2,1,0:T(8,128)(2,1)S(1)}) custom-call(bf16[32,256,512]{2,1,0:T(8,128)(2,1)} %chol.1, bf16[2048,1024]{1,0:T(8,128)(2,1)} %orbitals.1, bf16[1,1024,2048]{2,1,0:T(8,128)(2,1)} %greens.1), custom_call_target="tpu_custom_call" | custom-call | tf_op jit(solution)/shard_map/pallas_call | solution.py:263
  101.1 0.0 copy-done
  101.1 2.6 %shard_map.60 = (f32[1,4]{1,0:T(1,128)}, bf16[4,1024,512]{2,1,0:T(8,128)(2,1)}) custom-call(f32[1,4]{1,0:T(1,128)S(1)} %get-tuple-element.4.bias, f32[1,4]{1,0:T(1,128)S(1)} %bitcast.1, bf16[4,1024,512]{2,1,0:T(8,128)(2,1)S(1)} %get-tuple-element.5.rounded), custom_call_target="tpu_custom_call" | custom-call | tf_op jit(solution)/shard_map/pallas_call | solution.py:298
Async XLA Ops:
  0.6 100.4 %copy-start = (f32[4]{0:T(128)S(1)}, f32[4]{0:T(128)}, u32[]{:S(2)}) copy-start(f32[4]{0:T(128)} %param.7) | copy-start | bytes 52
